TPU v7x, 128 devices: a whole 4x4x4 slice. The times are simulated.
128 devices in a mesh: row: 32 (over z, y, core), col: 4 (over x).
Axes of the slice: x: 4, y: 4, z: 4, core: 2. Of those that a mesh axis runs over, the one named last changes fastest.
Arguments:
- tracer: float32 [512, 512, 512], P(None, 'row', 'col'), may hold values from -6 to 6
- symbol_x: float32 [512], replicated, may hold values from 0.3 to 3
- symbol_y: float32 [512], replicated, may hold values from 0.3 to 3
- symbol_z: float32 [512], replicated, may hold values from 0.3 to 3
Outputs:
- spectrum: float32 [512, 512, 512], P('row', 'col')
All inputs are finite; a program needn't handle non-finite values.
Results may differ from a plain program's by a relative error of at most 0.000075.
Values sent between devices are 32-bit elements; how exact they have to be, the bound alone decides.
A program may use at most 64 MiB of HBM per device.

v0:
```python
import jax
import jax.numpy as jnp
from jax import lax
from jax.sharding import PartitionSpec as P


def transform_table(count):
    rank = jnp.arange(count)
    angle = (
        jnp.pi
        / (count + 1)
        * ((rank[:, None] + 1) * (rank[None, :] + 1) % (2 * count + 2)).astype(jnp.float32)
    )
    return jnp.sin(angle) * (2.0 / (count + 1)) ** 0.5


def to_modes(values, dim):
    moved = jnp.tensordot(
        values,
        transform_table(values.shape[dim]),
        axes=([dim], [0]),
        precision=lax.Precision.HIGHEST,
    )
    return jnp.moveaxis(moved, -1, dim)


def per_device(tracer, symbol_x, symbol_y, symbol_z):
    part_values = tracer
    part_values = to_modes(part_values, 0)
    part_values = lax.all_to_all(part_values, "row", split_axis=0, concat_axis=1, tiled=True)
    part_values = to_modes(part_values, 1)
    local_values = part_values
    local_values = lax.all_to_all(local_values, "col", split_axis=1, concat_axis=2, tiled=True)
    local_values = to_modes(local_values, 2)
    share_x = local_values.shape[0]
    part_x = lax.dynamic_slice_in_dim(symbol_x, lax.axis_index("row") * share_x, share_x)
    share_y = local_values.shape[1]
    part_y = lax.dynamic_slice_in_dim(symbol_y, lax.axis_index("col") * share_y, share_y)
    symbol = part_x[:, None, None] + part_y[None, :, None] + symbol_z[None, None, :]
    local_values = local_values * ((1.0 - 0.2 * symbol) / (1.0 + 0.2 * symbol))
    return local_values


def solution(mesh):
    in_specs = (P(None, "row", "col"), P(), P(), P())
    out_specs = P("row", "col", None)
    return jax.shard_map(
        per_device, mesh=mesh, in_specs=in_specs, out_specs=out_specs, check_vma=False
    )
```

profile of v0, /device:TPU:1, one launch (start us, length us, event | category | flops | bytes accessed | tf_op | source)
XLA Modules:
  0.0 187.9 jit_solution(11608555901194596935)
XLA Ops:
  0.0 14.1 %fusion = f32[512,16,128]{2,0,1:T(8,128)S(1)} fusion(f32[512,16,128]{2,1,0:T(8,128)} %param.4, s32[512]{0:T(512)S(1)} %iota_add_fusion), kind=kOutput, calls=%fused_computation.1 | convolution fusion | flops 6445072384 | bytes 8390656 | tf_op jit(solution)/shard_map/dot_general | solution.py:18
  14.1 2.4 %copy.22 = f32[512,16,128]{2,1,0:T(8,128)S(1)} copy(f32[512,16,128]{2,0,1:T(8,128)S(1)} %fusion) | data formatting | bytes 8388608 | tf_op jit(solution)/shard_map/dot_general | solution.py:18
  16.6 60.2 %all_to_all.36 = f32[512,16,128]{2,1,0:T(8,128)S(1)} all-to-all(f32[512,16,128]{2,1,0:T(8,128)S(1)} %copy.22), channel_id=1, replica_groups=mesh['row'=32,'col'=4] {'row'}, dimensions={0} | all-to-all | bytes 8388608 | tf_op jit(solution)/shard_map/all_to_all | solution.py:30
  76.7 0.4 copy.23
  77.2 12.8 %convolution_bitcast_fusion = f32[16,512,128]{1,2,0:T(8,128)} fusion(f32[16,512,128]{2,1,0:T(8,128)S(1)} %bitcast.20, s32[512]{0:T(512)S(1)} %iota_add_fusion), kind=kOutput, calls=%fused_computation.4 | convolution fusion | flops 6445072384 | bytes 8390656 | tf_op jit(solution)/shard_map/dot_general | solution.py:18
  90.0 5.4 %copy.25 = f32[16,512,128]{2,0,1:T(8,128)} copy(f32[16,512,128]{1,2,0:T(8,128)} %convolution_bitcast_fusion) | data formatting | bytes 8388608 | tf_op jit(solution)/shard_map/transpose | solution.py:24
  95.5 15.5 %all-to-all-start.1 = ((f32[16,512,128]{2,0,1:T(8,128)}), f32[16,512,128]{2,0,1:T(8,128)}, u32[]{:S(2)}, u32[]{:S(2)}) async-start(f32[16,512,128]{2,0,1:T(8,128)} %copy.25), calls=%async_computation.1 | async-start | bytes 8388608 | tf_op jit(solution)/shard_map/all_to_all | solution.py:33
  111.0 0.8 dynamic_slice.7
  111.8 0.8 dynamic_slice.6
  112.5 0.1 broadcast_add_fusion
  112.6 47.0 %all-to-all-done.1 = f32[16,512,128]{2,0,1:T(8,128)} async-done(((f32[16,512,128]{2,0,1:T(8,128)}), f32[16,512,128]{2,0,1:T(8,128)}, u32[]{:S(2)}, u32[]{:S(2)}) %all-to-all-start.1) | async-done | bytes 4194336 | tf_op jit(solution)/shard_map/all_to_all | solution.py:33
  159.6 6.9 %copy.33 = f32[16,4,128,128]{3,1,2,0:T(4,128)} copy(f32[16,4,128,128]{3,0,2,1:T(8,128)} %bitcast.6) | data formatting | bytes 8388608 | tf_op jit(solution)/shard_map/all_to_all | solution.py:33
  166.5 0.0 copy-start
  166.5 5.5 %all_to_all.33 = f32[16,128,512]{2,1,0:T(8,128)} reshape(f32[16,128,4,128]{3,2,1,0:T(4,128)} %bitcast.19) | data formatting | bytes 8388608 | tf_op jit(solution)/shard_map/all_to_all | solution.py:33
  171.9 0.0 copy-done
  171.9 15.8 %divide_multiply_fusion = f32[16,128,512]{2,1,0:T(8,128)} fusion(f32[16,128,512]{2,1,0:T(8,128)} %all_to_all.33, f32[512]{0:T(512)S(1)} %copy-done, f32[16,128]{1,0:T(8,128)S(1)} %broadcast_add_fusion, s32[512]{0:T(512)S(1)} %iota_add_fusion), kind=kOutput, calls=%fused_computation.3 | convolution fusion | flops 6451363840 | bytes 8400896 | tf_op jit(solution)/shard_map/dot_general | solution.py:18
  (1 shorter events, 0.0 us)
Async XLA Ops:
  95.5 64.1 %all-to-all-start.1 = ((f32[16,512,128]{2,0,1:T(8,128)}), f32[16,512,128]{2,0,1:T(8,128)}, u32[]{:S(2)}, u32[]{:S(2)}) async-start(f32[16,512,128]{2,0,1:T(8,128)} %copy.25), calls=%async_computation.1 | async-start | bytes 8388608 | tf_op jit(solution)/shard_map/all_to_all | solution.py:33
  166.5 5.5 %copy-start = (f32[512]{0:T(512)S(1)}, f32[512]{0:T(512)}, u32[]{:S(2)}) copy-start(f32[512]{0:T(512)} %param.7) | copy-start | bytes 6148
where the time goes:
time: 192 us; the launch traced here: 188 us
  blocking collectives  60.2 us (31%)
  waiting for transfers between devices  47 us (24%)
  matrix products  42.7 us (22%)
  local copies, waits for them, and re-layouts  22.2 us (12%)
  starting transfers between devices  15.5 us (8%)
    all_to_all x1, blocking collectives, per_device(): lax.all_to_all(part_values, 'row', split_axis=0, concat_axis=1, tiled=True)  60.2 us
    all_to_all x1, waiting for transfers between devices, per_device(): lax.all_to_all(local_values, 'col', split_axis=1, concat_axis=2, tiled=True)  47 us
    dot_general x3, matrix products, to_modes(): jnp.tensordot(values, transform_table(values.shape[dim]), axes=([dim], [0...  42.7 us
    all_to_all x1, starting transfers between devices, per_device(): lax.all_to_all(local_values, 'col', split_axis=1, concat_axis=2, tiled=True)  15.5 us
    all_to_all x2, local copies, waits for them, and re-layouts, per_device(): lax.all_to_all(local_values, 'col', split_axis=1, concat_axis=2, tiled=True)  12.4 us
    transpose x1, local copies, waits for them, and re-layouts, to_modes(): return jnp.moveaxis(moved, -1, dim)  5.45 us
  transfers between devices with their start and end apart: 1, of which 1 were waited for; matrix products, arithmetic and copies ran while one was open for 1% of the time, Pallas kernels for 0%

commit v1 on v0

v1 whole, which is shorter than its diff:
```python
import functools

import jax
import jax.numpy as jnp
import numpy as np
from jax import lax
from jax.experimental import pallas as pl
from jax.experimental.pallas import tpu as pltpu
from jax.sharding import PartitionSpec as P

MESH = pl.DeviceIdType.MESH
PER_CHUNK = 1
AHEAD = 2


def transform_table(count):
    rank = np.arange(1, count + 1, dtype=np.int64)
    angle = (np.pi / (count + 1)) * ((rank[:, None] * rank[None, :]) % (2 * count + 2))
    return np.sin(angle) * np.sqrt(2.0 / (count + 1))


def halves(table):
    high = table.astype(jnp.bfloat16)
    low = (table - high.astype(np.float64)).astype(jnp.bfloat16)
    return high, low


def split(values):
    high = values.astype(jnp.bfloat16)
    return high, (values - high.astype(jnp.float32)).astype(jnp.bfloat16)


def dot(a, b):
    return jnp.dot(a, b, preferred_element_type=jnp.float32)


def kernel(
    rows,
    cols,
    field_hbm,
    table_x_hbm,
    table_hbm,
    symbol_x,
    symbol_y,
    symbol_z,
    out,
    field,
    high,
    low,
    table_x,
    table,
    outgoing,
    lines_y,
    turned,
    lines_z,
    field_sem,
    table_sem,
    row_send,
    row_recv,
    col_send,
    col_recv,
):
    row, col = lax.axis_index("row"), lax.axis_index("col")
    planes = field.shape[0]
    chunks, _, sent, wide = outgoing.shape
    per = sent // rows
    size_y = lines_y.shape[1]
    part_y = lines_z.shape[2]
    size = field.shape[1]

    barrier = pltpu.get_barrier_semaphore()

    def greet_row(step, _):
        pl.semaphore_signal(
            barrier, inc=1, device_id=(lax.rem(row + step, rows), col), device_id_type=MESH
        )
        return 0

    lax.fori_loop(1, rows, greet_row, 0)
    for step in range(1, cols):
        pl.semaphore_signal(
            barrier, inc=1, device_id=(row, lax.rem(col + step, cols)), device_id_type=MESH
        )

    load_x = pltpu.make_async_copy(table_x_hbm, table_x, table_sem.at[0])
    load_x.start()
    loads = [
        pltpu.make_async_copy(field_hbm.at[:, plane, :], field.at[plane], field_sem.at[plane])
        for plane in range(planes)
    ]
    for load in loads:
        load.start()
    load_table = pltpu.make_async_copy(table_hbm, table, table_sem.at[1])
    load_table.start()

    def along_x(chunk, pair):
        mine = table_x.at[chunk]
        both = dot(mine[...], high[pair])
        got = both[:sent] + both[sent:] + dot(mine[pl.ds(0, sent), :], low[pair])
        outgoing[chunk, 2 * pair] = got[:, :wide]
        outgoing[chunk, 2 * pair + 1] = got[:, wide:]

    def send_row(chunk):
        def to_peer(step, _):
            peer = lax.rem(row + step, rows)
            for mode in range(per):
                pltpu.make_async_remote_copy(
                    src_ref=outgoing.at[chunk, :, peer * per + mode, :],
                    dst_ref=lines_y.at[
                        chunk * per + mode, pl.ds(pl.multiple_of(row * planes, planes), planes), :
                    ],
                    send_sem=row_send,
                    recv_sem=row_recv.at[chunk],
                    device_id=(peer, col),
                    device_id_type=MESH,
                ).start()
            return 0

        lax.fori_loop(1, rows, to_peer, 0)
        for mode in range(per):
            for plane in range(planes):
                lines_y[chunk * per + mode, pl.ds(row * planes + plane, 1), :] = outgoing[
                    chunk, plane, pl.ds(row * per + mode, 1), :
                ]

    load_x.wait()
    for pair in range(planes // 2):
        loads[2 * pair].wait()
        loads[2 * pair + 1].wait()
        both = jnp.concatenate([field[2 * pair], field[2 * pair + 1]], axis=1)
        high[pair], low[pair] = split(both)
        along_x(0, pair)
    pl.semaphore_wait(barrier, rows - 1 + cols - 1)
    send_row(0)

    def next_chunk(chunk):
        for pair in range(planes // 2):
            along_x(chunk, pair)
        send_row(chunk)

    for chunk in range(1, AHEAD):
        next_chunk(chunk)
    load_table.wait()

    def along_y(chunk):
        arrived = lines_y.at[pl.ds(chunk * per, per), pl.ds(0, size_y - planes), :]
        pltpu.make_async_remote_copy(
            arrived, arrived, row_send, row_recv.at[chunk], device_id=(row, col), device_id_type=MESH
        ).wait_recv()
        for mode in range(per):
            above, below = split(lines_y[chunk * per + mode])
            got = dot(table[0], above) + dot(table[1], above) + dot(table[0], below)
            turned[chunk * per + mode] = got
        for step in range(1, cols):
            peer = lax.rem(col + step, cols)
            pltpu.make_async_remote_copy(
                src_ref=turned.at[
                    pl.ds(chunk * per, per), pl.ds(pl.multiple_of(peer * part_y, part_y), part_y), :
                ],
                dst_ref=lines_z.at[col, pl.ds(chunk * per, per)],
                send_sem=col_send,
                recv_sem=col_recv.at[chunk],
                device_id=(row, peer),
                device_id_type=MESH,
            ).start()
        for mode in range(per):
            lines_z[col, chunk * per + mode] = turned[
                chunk * per + mode, pl.ds(pl.multiple_of(col * part_y, part_y), part_y), :
            ]

    def along_z(chunk):
        arrived = lines_z.at[pl.ds(0, cols - 1), pl.ds(chunk * per, per)]
        pltpu.make_async_remote_copy(
            arrived, arrived, col_send, col_recv.at[chunk], device_id=(row, col), device_id_type=MESH
        ).wait_recv()
        for mode in range(per):
            at = chunk * per + mode
            line = jnp.concatenate([lines_z[part, at] for part in range(cols)], axis=1)
            above, below = split(line)
            got = dot(above, table[0]) + dot(above, table[1]) + dot(below, table[0])
            symbol = symbol_x[at] + symbol_y[...] + symbol_z[...]
            out[at] = got * (2.0 / (1.0 + 0.2 * symbol) - 1.0)

    def step(chunk, _):
        @pl.when(chunk + AHEAD < chunks)
        def _():
            next_chunk(chunk + AHEAD)

        along_y(chunk)

        @pl.when(chunk >= 1)
        def _():
            along_z(chunk - 1)

        return 0

    lax.fori_loop(0, chunks, step, 0)
    along_z(chunks - 1)
    all_rows = lines_y.at[:, pl.ds(0, size_y - planes), :]
    pltpu.make_async_remote_copy(
        all_rows, all_rows, row_send, row_recv.at[0], device_id=(row, col), device_id_type=MESH
    ).wait_send()
    all_cols = lines_z.at[pl.ds(0, cols - 1)]
    pltpu.make_async_remote_copy(
        all_cols, all_cols, col_send, col_recv.at[0], device_id=(row, col), device_id_type=MESH
    ).wait_send()


def per_device(rows, cols, field, symbol_x, symbol_y, symbol_z):
    size, planes, wide = field.shape
    size_y, size_z = planes * rows, wide * cols
    share, part_y = size // rows, size_y // cols
    per = PER_CHUNK
    chunks = share // per
    sent = rows * per

    high, low = halves(transform_table(size))
    order = np.arange(size).reshape(rows, chunks, per).transpose(1, 0, 2).reshape(chunks, sent)
    table_x = np.concatenate([high[order], low[order]], axis=1)
    table = np.stack([high, low])

    mine_x = lax.dynamic_slice_in_dim(symbol_x, lax.axis_index("row") * share, share)
    mine_y = lax.dynamic_slice_in_dim(symbol_y, lax.axis_index("col") * part_y, part_y)

    vmem = pl.BlockSpec(memory_space=pltpu.VMEM)
    anywhere = pl.BlockSpec(memory_space=pl.ANY)
    return pl.pallas_call(
        functools.partial(kernel, rows, cols),
        out_shape=jax.ShapeDtypeStruct((share, part_y, size_z), jnp.float32),
        in_specs=[anywhere, anywhere, anywhere, pl.BlockSpec(memory_space=pltpu.SMEM), vmem, vmem],
        out_specs=vmem,
        scratch_shapes=[
            pltpu.VMEM((planes, size, wide), jnp.float32),
            pltpu.VMEM((planes // 2, size, 2 * wide), jnp.bfloat16),
            pltpu.VMEM((planes // 2, size, 2 * wide), jnp.bfloat16),
            pltpu.VMEM(table_x.shape, jnp.bfloat16),
            pltpu.VMEM(table.shape, jnp.bfloat16),
            pltpu.VMEM((chunks, planes, sent, wide), jnp.float32),
            pltpu.VMEM((share, size_y, wide), jnp.float32),
            pltpu.VMEM((share, size_y, wide), jnp.float32),
            pltpu.VMEM((cols, share, part_y, wide), jnp.float32),
            pltpu.SemaphoreType.DMA((planes,)),
            pltpu.SemaphoreType.DMA((2,)),
            pltpu.SemaphoreType.DMA,
            pltpu.SemaphoreType.DMA((chunks,)),
            pltpu.SemaphoreType.DMA,
            pltpu.SemaphoreType.DMA((chunks,)),
        ],
        compiler_params=pltpu.CompilerParams(
            collective_id=0, has_side_effects=True, vmem_limit_bytes=60 << 20
        ),
        name="modes",
    )(
        field,
        jnp.asarray(table_x),
        jnp.asarray(table),
        mine_x,
        mine_y[:, None],
        symbol_z[None, :],
    )


def solution(mesh):
    rows, cols = mesh.shape["row"], mesh.shape["col"]
    return jax.shard_map(
        functools.partial(per_device, rows, cols),
        mesh=mesh,
        in_specs=(P(None, "row", "col"), P(), P(), P()),
        out_specs=P("row", "col", None),
        check_vma=False,
    )
```

time: 192 us -> 88.6 us (0.46); the launches traced: 188 us -> 88.4 us
  Pallas kernels: 0 us -> 80.8 us
  blocking collectives: 60.2 us -> 0 us
  waiting for transfers between devices: 47 us -> 0 us
  matrix products: 42.7 us -> 0 us
  starting transfers between devices: 15.5 us -> 0 us
  local copies, waits for them, and re-layouts: 22.2 us -> 7.59 us
    pallas_call x0 -> x1, Pallas kernels: none -> 80.8 us  [per_device(): pl.pallas_call(functools.partial(kernel, rows, cols), out_shape=jax.Shape...]
    all_to_all x1 -> x0, blocking collectives: 60.2 us -> none  [per_device(): lax.all_to_all(part_values, 'row', split_axis=0, concat_axis=1, tiled=True)]
    all_to_all x1 -> x0, waiting for transfers between devices: 47 us -> none  [per_device(): lax.all_to_all(local_values, 'col', split_axis=1, concat_axis=2, tiled=True)]
    dot_general x3 -> x0, matrix products: 42.7 us -> none  [to_modes(): jnp.tensordot(values, transform_table(values.shape[dim]), axes=([dim], [0...]
    all_to_all x1 -> x0, starting transfers between devices: 15.5 us -> none  [per_device(): lax.all_to_all(local_values, 'col', split_axis=1, concat_axis=2, tiled=True)]
    all_to_all x3 -> x0, local copies, waits for them, and re-layouts: 12.8 us -> none  [the longest x2 12.4 us: per_device(): lax.all_to_all(local_values, 'col', split_axis=1, concat_axis=2, tiled=True)]
    unnamed x2 -> x3, local copies, waits for them, and re-layouts: 0.01 us -> 5.49 us
    transpose x1 -> x0, local copies, waits for them, and re-layouts: 5.45 us -> none  [to_modes(): return jnp.moveaxis(moved, -1, dim)]
  transfers between devices with their start and end apart: 1 -> 0, of which waited for: 1 -> 0; matrix products, arithmetic and copies ran while one was open for 1% -> 0% of each run, Pallas kernels for 0% -> 0%
where the time goes in v1:
time: 88.6 us; the launch traced here: 88.4 us
  Pallas kernels  80.8 us (91%)
  local copies, waits for them, and re-layouts  7.59 us (9%)
    pallas_call x1, Pallas kernels, per_device(): pl.pallas_call(functools.partial(kernel, rows, cols), out_shape=jax.Shape...  80.8 us
    unnamed x3, local copies, waits for them, and re-layouts  5.49 us

profile of v1, /device:TPU:1, one launch (start us, length us, event | category | flops | bytes accessed | tf_op | source)
XLA Modules:
  0.0 88.4 jit_solution(16031912328376906193)
XLA Ops:
  0.0 0.0 copy-start
  0.0 0.7 copy-done
  0.7 0.1 dynamic-slice_bitcast_fusion
  0.8 1.3 %dynamic_slice.6.symbol_x = f32[16]{0:T(128)} dynamic-slice(f32[512]{0:T(512)} %param.7, s32[]{:T(128)S(6)} %select_n.6), dynamic_slice_sizes={16} | dynamic-slice | bytes 132 | tf_op jit(solution)/shard_map/dynamic_slice | solution.py:222
  2.1 0.7 copy.7.symbol_y
  2.8 80.8 %modes.1 = f32[16,128,512]{2,1,0:T(8,128)} custom-call(f32[512,16,128]{2,1,0:T(8,128)} %field_hbm.1, bf16[16,64,512]{2,1,0:T(8,128)(2,1)} %constant.21.clone.table_x_hbm, bf16[2,512,512]{2,1,0:T(8,128)(2,1)} %constant.22.clone.table_hbm, f32[16]{0:T(128)} %dynamic_slice.6.symbol_x, f32[128,1]{1,0:T(8,128)} %copy.7.symbol_y, f32[1,512]{1,0:T(1,128)} %bitcast.3), custom_call_target="tpu_custom_call" | custom-call | tf_op jit(solution)/shard_map/modes/pallas_call | solution.py:227
  83.6 4.8 %copy.9 = f32[16,128,512]{2,1,0:T(8,128)} copy(f32[16,128,512]{2,1,0:T(8,128)} %modes.1) | data formatting | bytes 8388608
Async XLA Ops:
  0.0 0.7 copy-start

commit v2 on v1

v2 whole, which is shorter than its diff:
```python
import functools

import jax
import jax.numpy as jnp
import numpy as np
from jax import lax
from jax.experimental import pallas as pl
from jax.experimental.pallas import tpu as pltpu
from jax.sharding import PartitionSpec as P

MESH = pl.DeviceIdType.MESH
GROUPS = 2
VMEM_LIMIT = 40 << 20


def transform_table(count):
    rank = np.arange(1, count + 1, dtype=np.int64)
    angle = (np.pi / (count + 1)) * ((rank[:, None] * rank[None, :]) % (2 * count + 2))
    return np.sin(angle) * np.sqrt(2.0 / (count + 1))


def halves(table):
    high = table.astype(jnp.bfloat16)
    low = (table - high.astype(np.float64)).astype(jnp.bfloat16)
    return high, low


def modes_of(share, groups):
    half = share // groups // 2
    order = []
    for group in range(groups):
        first = list(range(group * half, (group + 1) * half))
        order.append(first + [share - 1 - mode for mode in reversed(first)])
    return order


def split(values):
    high = values.astype(jnp.bfloat16)
    return high, (values - high.astype(jnp.float32)).astype(jnp.bfloat16)


def dot(a, b):
    return jnp.dot(a, b, preferred_element_type=jnp.float32)


def kernel(
    rows,
    cols,
    field_hbm,
    table_x_hbm,
    table_y_hbm,
    table_z_hbm,
    symbol_x_hbm,
    symbol_y_hbm,
    symbol_z_hbm,
    out,
    field,
    high,
    low,
    table_x,
    table_y,
    table_z,
    symbol_x,
    symbol_y,
    symbol_z,
    symbol_yz,
    outgoing,
    lines_y,
    turned,
    lines_z,
    field_sem,
    table_sem,
    row_send,
    row_recv,
    col_send,
    col_recv,
):
    row, col = lax.axis_index("row"), lax.axis_index("col")
    share, part_y, _ = out.shape
    planes, _, half, wide = field.shape
    groups, _, _, lots, _ = outgoing.shape
    size = 2 * half
    in_group = share // groups
    middle = rows // 2
    upper = row // middle
    place = pl.multiple_of((row + upper * (rows + middle - 1 - 2 * row)) * planes, planes)

    barrier = pltpu.get_barrier_semaphore()

    def greet_row(step, _):
        pl.semaphore_signal(
            barrier, inc=1, device_id=(lax.rem(row + step, rows), col), device_id_type=MESH
        )
        return 0

    loads = []
    load_x = pltpu.make_async_copy(table_x_hbm, table_x, table_sem.at[0])
    load_x.start()
    for plane in range(planes):
        source = plane + upper * (planes - 1 - 2 * plane)
        for parity in range(2):
            loads.append(
                pltpu.make_async_copy(
                    field_hbm.at[:, parity, source, :],
                    field.at[plane, parity],
                    field_sem.at[2 * plane + parity],
                )
            )
            loads[-1].start()
    later = [
        pltpu.make_async_copy(source, target, table_sem.at[1 + at])
        for at, (source, target) in enumerate(
            [
                (table_y_hbm, table_y),
                (table_z_hbm, table_z),
                (symbol_x_hbm, symbol_x),
                (symbol_y_hbm, symbol_y),
                (symbol_z_hbm, symbol_z),
            ]
        )
    ]
    for load in later:
        load.start()
    lax.fori_loop(1, rows, greet_row, 0)
    for step in range(1, cols):
        pl.semaphore_signal(
            barrier, inc=1, device_id=(row, lax.rem(col + step, cols)), device_id_type=MESH
        )

    def along_x(group, pair):
        parts = []
        for parity in range(2):
            mine = table_x.at[group, parity]
            both = dot(mine[...], high[pair, parity])
            parts.append(
                both[:lots] + both[lots:] + dot(mine[pl.ds(0, lots), :], low[pair, parity])
            )
        for sign, got in enumerate((parts[0] + parts[1], parts[0] - parts[1])):
            outgoing[group, sign, 2 * pair] = got[:, :wide]
            outgoing[group, sign, 2 * pair + 1] = got[:, wide:]

    def lot_of(chunk, peer):
        group, at = chunk // in_group, lax.rem(chunk, in_group)
        sign = peer // middle
        lot = (at + sign * (in_group - 1 - 2 * at)) * middle + peer + sign * (rows - 1 - 2 * peer)
        return group, sign, lot

    def send_row(chunk):
        def to_peer(step, _):
            peer = lax.rem(row + step, rows)
            group, sign, lot = lot_of(chunk, peer)
            pltpu.make_async_remote_copy(
                src_ref=outgoing.at[group, sign, :, lot, :],
                dst_ref=lines_y.at[chunk, pl.ds(place, planes), :],
                send_sem=row_send,
                recv_sem=row_recv.at[chunk],
                device_id=(peer, col),
                device_id_type=MESH,
            ).start()
            return 0

        lax.fori_loop(1, rows, to_peer, 0)
        group, sign, lot = lot_of(chunk, row)
        for plane in range(planes):
            lines_y[chunk, pl.ds(place + plane, 1), :] = outgoing[
                group, sign, plane, pl.ds(lot, 1), :
            ]

    load_x.wait()
    for pair in range(planes // 2):
        for parity in range(2):
            loads[4 * pair + parity].wait()
            loads[4 * pair + 2 + parity].wait()
            both = jnp.concatenate([field[2 * pair, parity], field[2 * pair + 1, parity]], axis=1)
            high[pair, parity], low[pair, parity] = split(both)
        along_x(0, pair)
    pl.semaphore_wait(barrier, rows - 1 + cols - 1)
    for chunk in range(in_group):
        send_row(chunk)

    for load in later:
        load.wait()
    mine_y = jnp.broadcast_to(
        symbol_y[:, pl.ds(pl.multiple_of(col * part_y, part_y), part_y)], (part_y, part_y)
    )
    symbol_yz[...] = jnp.transpose(mine_y)[:, :1] + symbol_z[...]

    def along_y(chunk):
        arrived = lines_y.at[chunk, pl.ds(0, size - planes), :]
        pltpu.make_async_remote_copy(
            arrived, arrived, row_send, row_recv.at[chunk], device_id=(row, col), device_id_type=MESH
        ).wait_recv()
        first, second = lines_y[chunk, pl.ds(0, half), :], lines_y[chunk, pl.ds(half, half), :]
        above, below = split(jnp.concatenate([first + second, first - second], axis=1))
        got = dot(table_y[0], above) + dot(table_y[1], above) + dot(table_y[0], below)
        turned[chunk, pl.ds(0, half, 2), :] = got[:half, :wide]
        turned[chunk, pl.ds(1, half, 2), :] = got[half:, wide:]
        for step in range(1, cols):
            peer = lax.rem(col + step, cols)
            pltpu.make_async_remote_copy(
                src_ref=turned.at[
                    chunk, pl.ds(pl.multiple_of(peer * part_y, part_y), part_y), :
                ],
                dst_ref=lines_z.at[col, chunk],
                send_sem=col_send,
                recv_sem=col_recv.at[chunk],
                device_id=(row, peer),
                device_id_type=MESH,
            ).start()
        lines_z[col, chunk] = turned[
            chunk, pl.ds(pl.multiple_of(col * part_y, part_y), part_y), :
        ]

    def along_z(chunk):
        arrived = lines_z.at[pl.ds(0, cols - 1), chunk]
        pltpu.make_async_remote_copy(
            arrived, arrived, col_send, col_recv.at[chunk], device_id=(row, col), device_id_type=MESH
        ).wait_recv()
        group, at = chunk // in_group, lax.rem(chunk, in_group)
        tail = at // (in_group // 2)
        mode = group * (in_group // 2) + at + tail * (share - in_group - group * in_group)
        above, below = split(jnp.concatenate([lines_z[part, chunk] for part in range(cols)], axis=1))
        got = dot(above, table_z[0]) + dot(above, table_z[1]) + dot(below, table_z[0])
        symbol = symbol_x[row * share + mode] + symbol_yz[...]
        out[mode] = got * (2.0 / (1.0 + 0.2 * symbol) - 1.0)

    def step(chunk, _):
        along_y(chunk)

        for group in range(1, groups):

            @pl.when(chunk == (group - 1) * in_group + 1)
            def _():
                for pair in range(planes // 2):
                    along_x(group, pair)

        @pl.when(jnp.logical_and(chunk >= 1, chunk + in_group - 1 < share))
        def _():
            send_row(chunk + in_group - 1)

        @pl.when(chunk >= 1)
        def _():
            along_z(chunk - 1)

        return 0

    lax.fori_loop(0, share, step, 0)
    along_z(share - 1)
    all_rows = lines_y.at[:, pl.ds(0, size - planes), :]
    pltpu.make_async_remote_copy(
        all_rows, all_rows, row_send, row_recv.at[0], device_id=(row, col), device_id_type=MESH
    ).wait_send()
    all_cols = lines_z.at[pl.ds(0, cols - 1)]
    pltpu.make_async_remote_copy(
        all_cols, all_cols, col_send, col_recv.at[0], device_id=(row, col), device_id_type=MESH
    ).wait_send()


def per_device(rows, cols, field, symbol_x, symbol_y, symbol_z):
    size, planes, wide = field.shape
    share, part_y = size // rows, size // cols
    half, middle = size // 2, rows // 2

    table = transform_table(size)
    high, low = halves(table)
    order = np.asarray(modes_of(share, GROUPS))
    lots = order.shape[1] * middle
    wanted = (order[:, :, None] + share * np.arange(middle)).reshape(GROUPS, lots)
    table_x = np.stack(
        [np.concatenate([part[wanted] for part in (high, low)], axis=1)[:, :, parity::2] for parity in (0, 1)],
        axis=1,
    )
    table_y = np.stack(
        [np.concatenate([part[0::2, :half], part[1::2, :half]]) for part in (high, low)]
    )
    table_z = np.stack([high, low])

    anywhere = pl.BlockSpec(memory_space=pl.ANY)
    return pl.pallas_call(
        functools.partial(kernel, rows, cols),
        out_shape=pltpu.VMEM((share, part_y, size), jnp.float32),
        in_specs=[anywhere] * 7,
        out_specs=pl.BlockSpec(memory_space=pltpu.VMEM),
        scratch_shapes=[
            pltpu.VMEM((planes, 2, half, wide), jnp.float32),
            pltpu.VMEM((planes // 2, 2, half, 2 * wide), jnp.bfloat16),
            pltpu.VMEM((planes // 2, 2, half, 2 * wide), jnp.bfloat16),
            pltpu.VMEM(table_x.shape, jnp.bfloat16),
            pltpu.VMEM(table_y.shape, jnp.bfloat16),
            pltpu.VMEM(table_z.shape, jnp.bfloat16),
            pltpu.SMEM((size,), jnp.float32),
            pltpu.VMEM((1, size), jnp.float32),
            pltpu.VMEM((1, size), jnp.float32),
            pltpu.VMEM((part_y, size), jnp.float32),
            pltpu.VMEM((GROUPS, 2, planes, lots, wide), jnp.float32),
            pltpu.VMEM((share, size, wide), jnp.float32),
            pltpu.VMEM((share, size, wide), jnp.float32),
            pltpu.VMEM((cols, share, part_y, wide), jnp.float32),
            pltpu.SemaphoreType.DMA((2 * planes,)),
            pltpu.SemaphoreType.DMA((6,)),
            pltpu.SemaphoreType.DMA,
            pltpu.SemaphoreType.DMA((share,)),
            pltpu.SemaphoreType.DMA,
            pltpu.SemaphoreType.DMA((share,)),
        ],
        compiler_params=pltpu.CompilerParams(
            collective_id=0, has_side_effects=True, vmem_limit_bytes=VMEM_LIMIT
        ),
        name="modes",
    )(
        *(
            pltpu.with_memory_space_constraint(operand, pltpu.HBM)
            for operand in (
                field.reshape(half, 2, planes, wide),
                jnp.asarray(table_x),
                jnp.asarray(table_y),
                jnp.asarray(table_z),
                symbol_x,
                symbol_y[None, :],
                symbol_z[None, :],
            )
        )
    )


def solution(mesh):
    rows, cols = mesh.shape["row"], mesh.shape["col"]
    return jax.shard_map(
        functools.partial(per_device, rows, cols),
        mesh=mesh,
        in_specs=(P(None, "row", "col"), P(), P(), P()),
        out_specs=P("row", "col", None),
        check_vma=False,
    )
```

time: 88.6 us -> 70.9 us (0.80)
  the two profiles are of different devices: /device:TPU:1 before, /device:TPU:24 now
where the time goes in v2:
time: 70.9 us; the launch traced here: 70.8 us
  Pallas kernels  68.8 us (97%)
  local copies, waits for them, and re-layouts  2.02 us (3%)
    pallas_call x1, Pallas kernels, per_device(): pl.pallas_call(functools.partial(kernel, rows, cols), out_shape=pltpu.VME...  68.8 us
    unnamed x1, local copies, waits for them, and re-layouts  2.02 us

profile of v2, /device:TPU:24, one launch (start us, length us, event | category | flops | bytes accessed | tf_op | source)
XLA Modules:
  0.0 70.8 jit_solution(17861643906263175001)
XLA Ops:
  0.0 68.8 %modes.1 = f32[16,128,512]{2,1,0:T(8,128)S(1)} custom-call(f32[256,2,16,128]{3,2,1,0:T(8,128)} %bitcast.3, bf16[2,2,256,256]{3,2,1,0:T(8,128)(2,1)} %constant.6.clone.table_x_hbm, bf16[2,512,256]{2,1,0:T(8,128)(2,1)} %constant.7.clone.table_y_hbm, bf16[2,512,512]{2,1,0:T(8,128)(2,1)} %constant.8.clone.table_z_hbm, f32[512]{0:T(512)} %symbol_x_hbm.1, ...), custom_call_target="tpu_custom_call" | custom-call | tf_op jit(solution)/shard_map/modes/pallas_call | solution.py:279
  68.8 2.0 %copy.9 = f32[16,128,512]{2,1,0:T(8,128)} copy(f32[16,128,512]{2,1,0:T(8,128)S(1)} %modes.1) | data formatting | bytes 8388608

commit v3 on v2

--- a/solution.py
+++ b/solution.py
@@ -1,4 +1,5 @@
 import functools
+import math
 
 import jax
 import jax.numpy as jnp
@@ -9,6 +10,8 @@
 from jax.sharding import PartitionSpec as P
 
 MESH = pl.DeviceIdType.MESH
+CORES = (1, 0)
+BEHIND = 3
 GROUPS = 2
 VMEM_LIMIT = 40 << 20
 
@@ -85,6 +88,18 @@
     upper = row // middle
     place = pl.multiple_of((row + upper * (rows + middle - 1 - 2 * row)) * planes, planes)
 
+    side = math.isqrt(middle)
+    chip, core = row // 2, lax.rem(row, 2)
+    peers = []
+    for target in CORES:
+        for ahead, across in sorted(
+            ((a, b) for a in range(side) for b in range(side)),
+            key=lambda at: -sum(min(step, side - step) for step in at),
+        )[:-1]:
+            there = lax.rem(chip // side + ahead, side) * side + lax.rem(chip + across, side)
+            peers.append(2 * there + target)
+    peers.append(2 * chip + 1 - core)
+
     barrier = pltpu.get_barrier_semaphore()
 
     def greet_row(step, _):
@@ -93,20 +108,23 @@
         )
         return 0
 
-    loads = []
+    def load_of(plane, parity, source):
+        return pltpu.make_async_copy(
+            field_hbm.at[:, parity, source, :],
+            field.at[plane, parity],
+            field_sem.at[2 * plane + parity],
+        )
+
     load_x = pltpu.make_async_copy(table_x_hbm, table_x, table_sem.at[0])
     load_x.start()
-    for plane in range(planes):
+
+    def load_plane(plane, _):
         source = plane + upper * (planes - 1 - 2 * plane)
         for parity in range(2):
-            loads.append(
-                pltpu.make_async_copy(
-                    field_hbm.at[:, parity, source, :],
-                    field.at[plane, parity],
-                    field_sem.at[2 * plane + parity],
-                )
-            )
-            loads[-1].start()
+            load_of(plane, parity, source).start()
+        return 0
+
+    lax.fori_loop(0, planes, load_plane, 0)
     later = [
         pltpu.make_async_copy(source, target, table_sem.at[1 + at])
         for at, (source, target) in enumerate(
@@ -145,23 +163,20 @@
         lot = (at + sign * (in_group - 1 - 2 * at)) * middle + peer + sign * (rows - 1 - 2 * peer)
         return group, sign, lot
 
-    def send_row(chunk):
-        def to_peer(step, _):
-            peer = lax.rem(row + step, rows)
+    def send_row(chunk, first=0, count=planes):
+        for peer in peers:
             group, sign, lot = lot_of(chunk, peer)
             pltpu.make_async_remote_copy(
-                src_ref=outgoing.at[group, sign, :, lot, :],
-                dst_ref=lines_y.at[chunk, pl.ds(place, planes), :],
+                src_ref=outgoing.at[group, sign, pl.ds(first, count), lot, :],
+                dst_ref=lines_y.at[chunk, pl.ds(place + first, count), :],
                 send_sem=row_send,
                 recv_sem=row_recv.at[chunk],
                 device_id=(peer, col),
                 device_id_type=MESH,
             ).start()
-            return 0
-
-        lax.fori_loop(1, rows, to_peer, 0)
+
         group, sign, lot = lot_of(chunk, row)
-        for plane in range(planes):
+        for plane in range(first, first + count):
             lines_y[chunk, pl.ds(place + plane, 1), :] = outgoing[
                 group, sign, plane, pl.ds(lot, 1), :
             ]
@@ -169,14 +184,21 @@
     load_x.wait()
     for pair in range(planes // 2):
         for parity in range(2):
-            loads[4 * pair + parity].wait()
-            loads[4 * pair + 2 + parity].wait()
+            load_of(2 * pair, parity, 2 * pair).wait()
+            load_of(2 * pair + 1, parity, 2 * pair + 1).wait()
             both = jnp.concatenate([field[2 * pair, parity], field[2 * pair + 1, parity]], axis=1)
             high[pair, parity], low[pair, parity] = split(both)
         along_x(0, pair)
-    pl.semaphore_wait(barrier, rows - 1 + cols - 1)
-    for chunk in range(in_group):
+        if pair == planes // 4 - 1:
+            pl.semaphore_wait(barrier, rows - 1 + cols - 1)
+            send_row(0, 0, planes // 2)
+    send_row(0, planes // 2, planes // 2)
+
+    def send_first(chunk, _):
         send_row(chunk)
+        return 0
+
+    lax.fori_loop(1, in_group, send_first, 0)
 
     for load in later:
         load.wait()
@@ -238,14 +260,19 @@
         def _():
             send_row(chunk + in_group - 1)
 
-        @pl.when(chunk >= 1)
+        @pl.when(chunk >= BEHIND)
         def _():
-            along_z(chunk - 1)
+            along_z(chunk - BEHIND)
 
         return 0
 
     lax.fori_loop(0, share, step, 0)
-    along_z(share - 1)
+
+    def last(chunk, _):
+        along_z(chunk)
+        return 0
+
+    lax.fori_loop(share - BEHIND, share, last, 0)
     all_rows = lines_y.at[:, pl.ds(0, size - planes), :]
     pltpu.make_async_remote_copy(
         all_rows, all_rows, row_send, row_recv.at[0], device_id=(row, col), device_id_type=MESH

time: 70.9 us -> 65.4 us (0.922)
  the two profiles are of different devices: /device:TPU:24 before, /device:TPU:1 now
where the time goes in v3:
time: 65.4 us; the launch traced here: 65 us
  Pallas kernels  63 us (96%)
  local copies, waits for them, and re-layouts  2.02 us (3%)
    pallas_call x1, Pallas kernels, per_device(): pl.pallas_call(functools.partial(kernel, rows, cols), out_shape=pltpu.VME...  63 us
    unnamed x1, local copies, waits for them, and re-layouts  2.02 us

profile of v3, /device:TPU:1, one launch (start us, length us, event | category | flops | bytes accessed | tf_op | source)
XLA Modules:
  0.0 65.0 jit_solution(10789851187725138102)
XLA Ops:
  0.0 63.0 %modes.1 = f32[16,128,512]{2,1,0:T(8,128)S(1)} custom-call(f32[256,2,16,128]{3,2,1,0:T(8,128)} %bitcast.3, bf16[2,2,256,256]{3,2,1,0:T(8,128)(2,1)} %constant.6.clone.table_x_hbm, bf16[2,512,256]{2,1,0:T(8,128)(2,1)} %constant.7.clone.table_y_hbm, bf16[2,512,512]{2,1,0:T(8,128)(2,1)} %constant.8.clone.table_z_hbm, f32[512]{0:T(512)} %symbol_x_hbm.1, ...), custom_call_target="tpu_custom_call" | custom-call | tf_op jit(solution)/shard_map/modes/pallas_call | solution.py:306
  63.0 2.0 %copy.9 = f32[16,128,512]{2,1,0:T(8,128)} copy(f32[16,128,512]{2,1,0:T(8,128)S(1)} %modes.1) | data formatting | bytes 8388608

commit v4 on v3

--- a/solution.py
+++ b/solution.py
@@ -12,7 +12,7 @@
 MESH = pl.DeviceIdType.MESH
 CORES = (1, 0)
 BEHIND = 3
-GROUPS = 2
+GROUPS = 4
 VMEM_LIMIT = 40 << 20
 
 
@@ -44,6 +44,30 @@
 
 def dot(a, b):
     return jnp.dot(a, b, preferred_element_type=jnp.float32)
+
+
+def lines_along_z(lines, chunk, table):
+    above, below = split(
+        jnp.concatenate([lines[part, chunk] for part in range(lines.shape[0])], axis=1)
+    )
+    return dot(above, table[0]) + dot(above, table[1]) + dot(below, table[0])
+
+
+def put(values, lines, table, factor, out, last, sem):
+    share = values.shape[0]
+    final = modes_of(share, GROUPS)[-1][-1]
+    copies = [
+        pltpu.make_async_copy(values.at[mode], out.at[mode], sem.at[mode])
+        for mode in range(share)
+        if mode != final
+    ]
+    for copy in copies:
+        copy.start()
+    last[...] = lines_along_z(lines, share - 1, table) * factor[...]
+    copies.append(pltpu.make_async_copy(last, out.at[final], sem.at[final]))
+    copies[-1].start()
+    for copy in copies:
+        copy.wait()
 
 
 def kernel(
@@ -57,12 +81,14 @@
     symbol_y_hbm,
     symbol_z_hbm,
     out,
+    lines_z,
+    table_z,
+    factor,
     field,
     high,
     low,
     table_x,
     table_y,
-    table_z,
     symbol_x,
     symbol_y,
     symbol_z,
@@ -70,7 +96,6 @@
     outgoing,
     lines_y,
     turned,
-    lines_z,
     field_sem,
     table_sem,
     row_send,
@@ -79,6 +104,15 @@
     col_recv,
 ):
     row, col = lax.axis_index("row"), lax.axis_index("col")
+    barrier = pltpu.get_barrier_semaphore()
+    for step in range(1, rows):
+        pl.semaphore_signal(
+            barrier, inc=1, device_id=(lax.rem(row + step, rows), col), device_id_type=MESH
+        )
+    for step in range(1, cols):
+        pl.semaphore_signal(
+            barrier, inc=1, device_id=(row, lax.rem(col + step, cols)), device_id_type=MESH
+        )
     share, part_y, _ = out.shape
     planes, _, half, wide = field.shape
     groups, _, _, lots, _ = outgoing.shape
@@ -100,13 +134,6 @@
             peers.append(2 * there + target)
     peers.append(2 * chip + 1 - core)
 
-    barrier = pltpu.get_barrier_semaphore()
-
-    def greet_row(step, _):
-        pl.semaphore_signal(
-            barrier, inc=1, device_id=(lax.rem(row + step, rows), col), device_id_type=MESH
-        )
-        return 0
 
     def load_of(plane, parity, source):
         return pltpu.make_async_copy(
@@ -139,12 +166,6 @@
     ]
     for load in later:
         load.start()
-    lax.fori_loop(1, rows, greet_row, 0)
-    for step in range(1, cols):
-        pl.semaphore_signal(
-            barrier, inc=1, device_id=(row, lax.rem(col + step, cols)), device_id_type=MESH
-        )
-
     def along_x(group, pair):
         parts = []
         for parity in range(2):
@@ -217,8 +238,8 @@
         got = dot(table_y[0], above) + dot(table_y[1], above) + dot(table_y[0], below)
         turned[chunk, pl.ds(0, half, 2), :] = got[:half, :wide]
         turned[chunk, pl.ds(1, half, 2), :] = got[half:, wide:]
-        for step in range(1, cols):
-            peer = lax.rem(col + step, cols)
+        for step in range(cols - 1):
+            peer = step + (col <= step).astype(jnp.int32)
             pltpu.make_async_remote_copy(
                 src_ref=turned.at[
                     chunk, pl.ds(pl.multiple_of(peer * part_y, part_y), part_y), :
@@ -233,18 +254,21 @@
             chunk, pl.ds(pl.multiple_of(col * part_y, part_y), part_y), :
         ]
 
-    def along_z(chunk):
+    def wait_col(chunk):
         arrived = lines_z.at[pl.ds(0, cols - 1), chunk]
         pltpu.make_async_remote_copy(
             arrived, arrived, col_send, col_recv.at[chunk], device_id=(row, col), device_id_type=MESH
         ).wait_recv()
+
+    def factor_of(mode):
+        return 2.0 / (1.0 + 0.2 * (symbol_x[row * share + mode] + symbol_yz[...])) - 1.0
+
+    def along_z(chunk):
+        wait_col(chunk)
         group, at = chunk // in_group, lax.rem(chunk, in_group)
         tail = at // (in_group // 2)
         mode = group * (in_group // 2) + at + tail * (share - in_group - group * in_group)
-        above, below = split(jnp.concatenate([lines_z[part, chunk] for part in range(cols)], axis=1))
-        got = dot(above, table_z[0]) + dot(above, table_z[1]) + dot(below, table_z[0])
-        symbol = symbol_x[row * share + mode] + symbol_yz[...]
-        out[mode] = got * (2.0 / (1.0 + 0.2 * symbol) - 1.0)
+        out[mode] = lines_along_z(lines_z, chunk, table_z) * factor_of(mode)
 
     def step(chunk, _):
         along_y(chunk)
@@ -272,7 +296,9 @@
         along_z(chunk)
         return 0
 
-    lax.fori_loop(share - BEHIND, share, last, 0)
+    factor[...] = factor_of(modes_of(share, groups)[-1][-1])
+    lax.fori_loop(share - BEHIND, share - 1, last, 0)
+    wait_col(share - 1)
     all_rows = lines_y.at[:, pl.ds(0, size - planes), :]
     pltpu.make_async_remote_copy(
         all_rows, all_rows, row_send, row_recv.at[0], device_id=(row, col), device_id_type=MESH
@@ -303,18 +329,23 @@
     table_z = np.stack([high, low])
 
     anywhere = pl.BlockSpec(memory_space=pl.ANY)
-    return pl.pallas_call(
+    vmem = pl.BlockSpec(memory_space=pltpu.VMEM)
+    made = pl.pallas_call(
         functools.partial(kernel, rows, cols),
-        out_shape=pltpu.VMEM((share, part_y, size), jnp.float32),
+        out_shape=(
+            pltpu.VMEM((share, part_y, size), jnp.float32),
+            pltpu.VMEM((cols, share, part_y, wide), jnp.float32),
+            pltpu.VMEM(table_z.shape, jnp.bfloat16),
+            pltpu.VMEM((part_y, size), jnp.float32),
+        ),
         in_specs=[anywhere] * 7,
-        out_specs=pl.BlockSpec(memory_space=pltpu.VMEM),
+        out_specs=(vmem,) * 4,
         scratch_shapes=[
             pltpu.VMEM((planes, 2, half, wide), jnp.float32),
             pltpu.VMEM((planes // 2, 2, half, 2 * wide), jnp.bfloat16),
             pltpu.VMEM((planes // 2, 2, half, 2 * wide), jnp.bfloat16),
             pltpu.VMEM(table_x.shape, jnp.bfloat16),
             pltpu.VMEM(table_y.shape, jnp.bfloat16),
-            pltpu.VMEM(table_z.shape, jnp.bfloat16),
             pltpu.SMEM((size,), jnp.float32),
             pltpu.VMEM((1, size), jnp.float32),
             pltpu.VMEM((1, size), jnp.float32),
@@ -322,7 +353,6 @@
             pltpu.VMEM((GROUPS, 2, planes, lots, wide), jnp.float32),
             pltpu.VMEM((share, size, wide), jnp.float32),
             pltpu.VMEM((share, size, wide), jnp.float32),
-            pltpu.VMEM((cols, share, part_y, wide), jnp.float32),
             pltpu.SemaphoreType.DMA((2 * planes,)),
             pltpu.SemaphoreType.DMA((6,)),
             pltpu.SemaphoreType.DMA,
@@ -348,6 +378,18 @@
             )
         )
     )
+    return pl.pallas_call(
+        put,
+        out_shape=pltpu.HBM((share, part_y, size), jnp.float32),
+        in_specs=[vmem] * 4,
+        out_specs=pl.BlockSpec(memory_space=pltpu.HBM),
+        scratch_shapes=[
+            pltpu.VMEM((part_y, size), jnp.float32),
+            pltpu.SemaphoreType.DMA((share,)),
+        ],
+        compiler_params=pltpu.CompilerParams(vmem_limit_bytes=8 << 20),
+        name="put",
+    )(*(pltpu.with_memory_space_constraint(part, pltpu.VMEM) for part in made))
 
 
 def solution(mesh):

time: 65.4 us -> 65 us (level)
  local copies, waits for them, and re-layouts: 2.02 us -> 0 us
  Pallas kernels: 63 us -> 64.9 us
    unnamed x1 -> x0, local copies, waits for them, and re-layouts: 2.02 us -> none
    pallas_call x1 -> x2, Pallas kernels: 63 us -> 64.9 us  [the longest x1 62.7 us: per_device(): pl.pallas_call(functools.partial(kernel, rows, cols), out_shape=(pltpu.VM...]
where the time goes in v4:
time: 65 us; the launch traced here: 64.9 us
  Pallas kernels  64.9 us (100%)
    pallas_call x1, Pallas kernels, per_device(): pl.pallas_call(functools.partial(kernel, rows, cols), out_shape=(pltpu.VM...  62.7 us
    pallas_call x1, Pallas kernels, per_device(): pl.pallas_call(put, out_shape=pltpu.HBM((share, part_y, size), jnp.float3...  2.15 us

profile of v4, /device:TPU:1, one launch (start us, length us, event | category | flops | bytes accessed | tf_op | source)
XLA Modules:
  0.0 64.9 jit_solution(239354425708042722)
XLA Ops:
  0.0 62.7 %modes.1 = (f32[16,128,512]{2,1,0:T(8,128)S(1)}, f32[4,16,128,128]{3,2,1,0:T(8,128)S(1)}, bf16[2,512,512]{2,1,0:T(8,128)(2,1)S(1)}, f32[128,512]{1,0:T(8,128)S(1)}) custom-call(f32[256,2,16,128]{3,2,1,0:T(8,128)} %bitcast.3, bf16[4,2,128,256]{3,2,1,0:T(8,128)(2,1)} %constant.6.clone.table_x_hbm, bf16[2,512,256]{2,1,0:T(8,128)(2,1)} %constant.7.clone.table_y_hbm, ...), custom_call_target="tpu_custom_call" | custom-call | tf_op jit(solution)/shard_map/modes/pallas_call | solution.py:333
  62.7 2.1 %put.1 = f32[16,128,512]{2,1,0:T(8,128)} custom-call(f32[16,128,512]{2,1,0:T(8,128)S(1)} %get-tuple-element.9.values, f32[4,16,128,128]{3,2,1,0:T(8,128)S(1)} %get-tuple-element.10.lines, bf16[2,512,512]{2,1,0:T(8,128)(2,1)S(1)} %get-tuple-element.11.table, f32[128,512]{1,0:T(8,128)S(1)} %get-tuple-element.12.factor), custom_call_target="tpu_custom_call" | custom-call | tf_op jit(solution)/shard_map/put/pallas_call | solution.py:381
